TPU v7x, 32 devices: a whole 2x2x4 slice. The times are simulated.
32 devices in a mesh: dp: 2 (over x), tp: 4 (over z), fsdp: 4 (over y, core).
Axes of the slice: x: 2, y: 2, z: 4, core: 2. Of those that a mesh axis runs over, the one named last changes fastest.
Arguments:
- x_in: bfloat16 [8, 2048, 3072], P(('dp', 'fsdp')), parts along dimension 0
- seq_lens: int32 [8], P(('dp', 'fsdp')), parts along dimension 0
- ln1_gain: bfloat16 [3072], replicated
- w_q: bfloat16 [3072, 32, 128], P('fsdp', 'tp')
- w_k: bfloat16 [3072, 8, 128], P('fsdp', 'tp')
- w_v: bfloat16 [3072, 8, 128], P('fsdp', 'tp')
- w_o: bfloat16 [32, 128, 3072], P('tp', None, 'fsdp')
- ln2_gain: bfloat16 [3072], replicated
- w_up: bfloat16 [3072, 9216], P('fsdp', 'tp')
- w_down: bfloat16 [9216, 3072], P('tp', 'fsdp')
Outputs:
- output 1: bfloat16 [8, 2048, 3072], P(('dp', 'fsdp')), parts along dimension 0
- output 2: bfloat16 [8, 2048, 8, 128], P(('dp', 'fsdp'), None, 'tp'), parts along dimension 0
- output 3: bfloat16 [8, 2048, 8, 128], P(('dp', 'fsdp'), None, 'tp'), parts along dimension 0
There are 2 independent parts. A program takes and returns all parts, laid end to end along the dimension named above; an argument that names none is the same for every part.
All inputs are finite; a program needn't handle non-finite values.
Results may differ from a plain program's by a relative error of at most 0.02.
Values are sent between devices in bfloat16 or wider.
A program may use at most 1 GiB of HBM per device.

v0:
```python
import functools

import jax
import jax.numpy as jnp
from jax import lax
from jax.experimental import pallas as pl
from jax.experimental.pallas import tpu as pltpu
from jax.sharding import PartitionSpec as P

EPS = 1e-5
ROPE_BASE = 10000.0
PIECES = 16
PER_GROUP = 4
TILE = 256
QBLK = 256
KBLK = 512

def layer_norm(x_rows, gain_vec):
    x_f32 = x_rows.astype(jnp.float32)
    mean_x = jnp.mean(x_f32, axis=-1, keepdims=True)
    centred = x_f32 - mean_x
    var_x = jnp.mean(centred * centred, axis=-1, keepdims=True)
    return (centred * lax.rsqrt(var_x + EPS) * (1.0 + gain_vec.astype(jnp.float32))).astype(jnp.bfloat16)


def rotary_tables(seq_length, head_dim):
    rot_dims = head_dim // 2
    half_rot = rot_dims // 2
    inv_freq = ROPE_BASE ** (-2.0 * jnp.arange(half_rot, dtype=jnp.float32) / rot_dims)
    angles = jnp.arange(seq_length, dtype=jnp.float32)[:, None] * inv_freq[None, :]
    cos_t, sin_t = jnp.cos(angles), jnp.sin(angles)
    zeros = jnp.zeros_like(sin_t)
    tail = jnp.zeros((seq_length, head_dim - rot_dims), jnp.float32)
    keep = jnp.concatenate([cos_t, cos_t, tail + 1.0], axis=1)
    from_low = jnp.concatenate([zeros, sin_t, tail], axis=1)
    from_high = jnp.concatenate([-sin_t, zeros, tail], axis=1)
    return keep, from_low, from_high


def rotate(t_bf16, keep, from_low, from_high):
    head_dim = t_bf16.shape[1]
    quarter = head_dim // 4
    t_f32 = t_bf16.astype(jnp.float32)
    low = pltpu.roll(t_f32, quarter, 1)
    high = pltpu.roll(t_f32, head_dim - quarter, 1)
    return (t_f32 * keep + low * from_low + high * from_high).astype(jnp.bfloat16)


def strip_attention(q_rot, k_blocks, v_blocks, row0, seq_len):
    head_dim = q_rot[0].shape[1]
    scale = head_dim ** -0.5

    def step(diagonal, kb, carry):
        start = pl.multiple_of(kb * KBLK, KBLK)
        k_blk = k_blocks(start)
        v_blk = v_blocks(start)
        length_bias = jnp.where(start + lax.broadcasted_iota(jnp.int32, (1, KBLK), 1) < seq_len, 0.0, -1e30)
        if diagonal:
            rows = row0 + lax.broadcasted_iota(jnp.int32, (QBLK, KBLK), 0)
            cols = start + lax.broadcasted_iota(jnp.int32, (QBLK, KBLK), 1)
            causal = cols <= rows
        out = []
        for q_head, (m_old, l_old, acc) in zip(q_rot, carry):
            s = lax.dot_general(q_head, k_blk, (((1,), (1,)), ((), ())), preferred_element_type=jnp.float32) * scale + length_bias
            if diagonal:
                s = jnp.where(causal, s, -1e30)
            m_new = jnp.maximum(m_old, jnp.max(s, axis=1, keepdims=True))
            corr = jnp.exp(m_old - m_new)
            p = jnp.exp(s - m_new)
            l_new = l_old * corr + jnp.sum(p, axis=1, keepdims=True)
            acc = acc * corr + jnp.dot(p.astype(jnp.bfloat16), v_blk, preferred_element_type=jnp.float32)
            out.append((m_new, l_new, acc))
        return tuple(out)

    carry = tuple(
        (jnp.full((QBLK, 1), -1e30, jnp.float32), jnp.zeros((QBLK, 1), jnp.float32), jnp.zeros((QBLK, head_dim), jnp.float32))
        for _ in q_rot
    )
    carry = lax.fori_loop(0, row0 // KBLK, functools.partial(step, False), carry)
    carry = lax.fori_loop(row0 // KBLK, (row0 + QBLK + KBLK - 1) // KBLK, functools.partial(step, True), carry)
    return [(acc / l_sum).astype(jnp.bfloat16) for _, l_sum, acc in carry]


def first_strips_kernel(len_ref, q_ref, k_ref, v_ref, qc_ref, ql_ref, qh_ref, kc_ref, kl_ref, kh_ref, ctx_ref, k_rot_ref):
    head_dim = k_ref.shape[1]

    @pl.when(pl.program_id(1) == 0)
    def _():
        k_rot_ref[...] = rotate(k_ref[...], kc_ref[...], kl_ref[...], kh_ref[...])

    tables = (qc_ref[...], ql_ref[...], qh_ref[...])
    heads = range(0, q_ref.shape[1], head_dim)
    context = strip_attention(
        [rotate(q_ref[:, h:h + head_dim], *tables) for h in heads],
        lambda start: k_rot_ref[pl.ds(start, KBLK), :],
        lambda start: v_ref[pl.ds(start, KBLK), :],
        pl.program_id(1) * (k_ref.shape[0] // 2),
        len_ref[0],
    )
    for h, rows in zip(heads, context):
        ctx_ref[:, h:h + head_dim] = rows


def first_strips(qkv, seq_lens, tables, q_heads, kv_heads, head_dim):
    seq_length = qkv.shape[0]
    width = q_heads // kv_heads * head_dim
    strips = seq_length // 2 // QBLK
    table_q = pl.BlockSpec((QBLK, head_dim), lambda g, i, *_: (i * strips, 0))
    table_k = pl.BlockSpec((seq_length, head_dim), lambda g, i, *_: (0, 0))
    return pl.pallas_call(
        first_strips_kernel,
        grid_spec=pltpu.PrefetchScalarGridSpec(
            num_scalar_prefetch=1,
            grid=(kv_heads, 2),
            in_specs=[
                pl.BlockSpec((QBLK, width), lambda g, i, *_: (i * strips, g)),
                pl.BlockSpec((seq_length, head_dim), lambda g, i, *_: (0, q_heads + g)),
                pl.BlockSpec((seq_length, head_dim), lambda g, i, *_: (0, q_heads + kv_heads + g)),
            ] + [table_q] * 3 + [table_k] * 3,
            out_specs=[
                pl.BlockSpec((QBLK, width), lambda g, i, *_: (i, g)),
                pl.BlockSpec((seq_length, head_dim), lambda g, i, *_: (0, g)),
            ],
        ),
        out_shape=[
            jax.ShapeDtypeStruct((2 * QBLK, q_heads * head_dim), jnp.bfloat16),
            jax.ShapeDtypeStruct((seq_length, kv_heads * head_dim), jnp.bfloat16),
        ],
        compiler_params=pltpu.CompilerParams(dimension_semantics=("arbitrary", "arbitrary"), vmem_limit_bytes=48 << 20),
        cost_estimate=pl.CostEstimate(flops=15 * 10 ** 9, bytes_accessed=12 << 20, transcendentals=0),
        name="first_strips",
    )(seq_lens, qkv, qkv, qkv, *tables, *tables)


class Line:
    def __init__(self, n_tp, half):
        self.z = lax.axis_index("tp")
        self.others = (lax.axis_index("dp"), lax.axis_index("fsdp"))
        self.last = n_tp - 1
        self.place = (self.z, self.last - self.z)
        self.sum_base = (half, 0)
        self.row_base = (0, half)

    def device(self, d):
        return (self.others[0], self.z + (1 if d == 0 else -1), self.others[1])

    def copy(self, d, src, dst, send_sem, recv_sem):
        return pltpu.make_async_remote_copy(
            src_ref=src, dst_ref=dst, send_sem=send_sem, recv_sem=recv_sem,
            device_id=self.device(d), device_id_type=pl.DeviceIdType.MESH,
        )

    def meet(self):
        barrier = pltpu.get_barrier_semaphore()
        for d in range(2):

            @pl.when(self.place[d] < self.last)
            def _():
                pl.semaphore_signal(barrier, inc=1, device_id=self.device(d), device_id_type=pl.DeviceIdType.MESH)

        pl.semaphore_wait(barrier, sum((place < self.last).astype(jnp.int32) for place in self.place))


def own_copies(line, half, pairs):
    for d in range(2):

        @pl.when(line.place[d] == line.last)
        def _():
            pairs(d, line.sum_base[d])


def sum_step(line, d, p, rows, part_ref, sum_ref, send, recv, finish):
    here = pl.ds(pl.multiple_of(p * rows, rows), rows)
    part_rows = pl.ds(pl.multiple_of(line.sum_base[d] + p * rows, rows), rows)
    place = line.place[d]

    @pl.when(place == 0)
    def _():
        line.copy(d, part_ref.at[part_rows], sum_ref.at[d, here], send.at[d, p], recv.at[d, p]).start()

    @pl.when(place > 0)
    def _():
        copy = line.copy(d, sum_ref.at[d, here], sum_ref.at[d, here], send.at[d, p], recv.at[d, p])
        copy.wait_recv()
        total = sum_ref[d, here, :].astype(jnp.float32) + part_ref[part_rows, :].astype(jnp.float32)

        @pl.when(place < line.last)
        def _():
            sum_ref[d, here, :] = total.astype(jnp.bfloat16)
            copy.start()

        @pl.when(place == line.last)
        def _():
            rows_done = (sum_ref[1 - d, here, :].astype(jnp.float32) + total).astype(jnp.bfloat16)
            sum_ref[d, here, :] = rows_done
            finish(here, part_rows, rows_done)


def drain_sums(line, rows, part_ref, sum_ref, send, recv, finished):
    def body(p, _):
        here = pl.ds(pl.multiple_of(p * rows, rows), rows)
        for d in range(2):

            @pl.when(line.place[d] < line.last)
            def _():
                line.copy(d, sum_ref.at[d, here], sum_ref.at[d, here], send.at[d, p], recv.at[d, p]).wait_send()

            @pl.when(line.place[d] == line.last)
            def _():
                finished(d, p, here)

        return 0

    lax.fori_loop(0, PIECES, body, 0)


def attend_reduce_kernel(n_tp, q_heads, len_ref, qkv, k_rot, keep, from_low, from_high, gain_ref, first_hbm, o_hbm, x_hbm,
                         x_own_hbm, h_own_hbm, o_full, part, sums, ctx, load_sem, x_sem, send, recv, x_out, h_out):
    half = part.shape[0] // 2
    rows = half // PIECES
    strips = half // QBLK
    per_strip = PIECES // strips
    head_dim = keep.shape[1]
    kv_heads = k_rot.shape[1] // head_dim
    group = q_heads // kv_heads
    line = Line(n_tp, half)
    loads = (pltpu.make_async_copy(first_hbm, ctx, load_sem.at[0]), pltpu.make_async_copy(o_hbm, o_full, load_sem.at[1]))
    for load in loads:
        load.start()

    def own(d, row):
        return pltpu.make_async_copy(x_hbm.at[pl.ds(row, half)], sums.at[1 - d], x_sem)

    own_copies(line, half, lambda d, row: own(d, row).start())
    line.meet()
    for load in loads:
        load.wait()
    seq_len = len_ref[0]

    def lanes_of(index, size):
        return pl.ds(pl.multiple_of(index * size, size), size)

    def output_product(strip):
        def tile(n, _):
            lanes = lanes_of(n, TILE)
            for k in range(2):
                product = jnp.dot(ctx[k * QBLK:(k + 1) * QBLK, :], o_full[:, lanes], preferred_element_type=jnp.float32)
                part[pl.ds(pl.multiple_of(k * half + strip * QBLK, QBLK), QBLK), lanes] = product.astype(jnp.bfloat16)
            return 0

        lax.fori_loop(0, part.shape[1] // TILE, tile, 0)

    def attend(strip, k, kv):
        row0 = pl.multiple_of(k * half + strip * QBLK, QBLK)
        q_rows = pl.ds(row0, QBLK)
        tables = (keep[q_rows, :], from_low[q_rows, :], from_high[q_rows, :])
        context = strip_attention(
            [rotate(qkv[q_rows, lanes_of(kv * group + h, head_dim)], *tables) for h in range(group)],
            lambda start: k_rot[pl.ds(start, KBLK), lanes_of(kv, head_dim)],
            lambda start: qkv[pl.ds(start, KBLK), lanes_of(q_heads + kv_heads + kv, head_dim)],
            row0,
            seq_len,
        )
        for h in range(group):
            ctx[pl.ds(pl.multiple_of(k * QBLK, QBLK), QBLK), lanes_of(kv * group + h, head_dim)] = context[h]

    output_product(0)
    own_copies(line, half, lambda d, row: own(d, row).wait())

    def outward(d, p, here):
        part_rows = pl.ds(pl.multiple_of(line.sum_base[d] + p * rows, rows), rows)
        return (
            pltpu.make_async_copy(sums.at[d, here], x_own_hbm.at[here], x_out.at[p]),
            pltpu.make_async_copy(part.at[part_rows], h_own_hbm.at[here], h_out.at[p]),
        )

    def step(t, _):
        for d in range(2):
            p = t - line.place[d]

            def finish(here, part_rows, rows_done, d=d, p=p):
                part[part_rows, :] = layer_norm(rows_done, gain_ref[...])
                for copy in outward(d, p, here):
                    copy.start()

            @pl.when((p >= 0) & (p < PIECES))
            def _():
                sum_step(line, d, p, rows, part, sums, send, recv, finish)

        strip = t // per_strip + 1
        unit = t % per_strip

        @pl.when(strip < strips)
        def _():
            @pl.when(unit < 2 * kv_heads)
            def _():
                attend(strip, unit // kv_heads, unit % kv_heads)

            @pl.when(unit == per_strip - 1)
            def _():
                output_product(strip)

        return 0

    lax.fori_loop(0, PIECES + line.last, step, 0)

    def finished(d, p, here):
        for copy in outward(d, p, here):
            copy.wait()

    drain_sums(line, rows, part, sums, send, recv, finished)


def mlp_kernel(n_tp, x_own_hbm, h_own_hbm, up_hbm, down_hbm, out_hbm, up, down, h, sums, act,
               w_sem, own_sem, h_send, h_recv, send, recv, y_send, y_recv, y_out):
    half = h.shape[0] // 2
    rows = half // PIECES
    group_rows = rows * PER_GROUP
    groups = PIECES // PER_GROUP
    up_tiles, down_tiles = up.shape[1] // TILE, down.shape[1] // TILE
    per_step = pl.cdiv(up_tiles + down_tiles, PER_GROUP)
    line = Line(n_tp, half)
    first = PER_GROUP + line.last
    loads = (pltpu.make_async_copy(up_hbm, up, w_sem.at[0]), pltpu.make_async_copy(down_hbm, down, w_sem.at[1]))

    def own(d, row):
        return (
            pltpu.make_async_copy(x_own_hbm, sums.at[1 - d], own_sem.at[0]),
            pltpu.make_async_copy(h_own_hbm, h.at[pl.ds(row, half)], own_sem.at[1]),
        )

    own_copies(line, half, lambda d, row: [c.start() for c in own(d, row)])
    for load in loads:
        load.start()
    line.meet()
    own_copies(line, half, lambda d, row: [c.wait() for c in own(d, row)])

    def row_slice(d, p):
        return pl.ds(pl.multiple_of(line.row_base[d] + p * rows, rows), rows)

    def h_copy(d, p):
        return line.copy(d, h.at[row_slice(d, p)], h.at[row_slice(d, p)], h_send.at[d, p], h_recv.at[d, p])

    def y_local(d, p, here):
        return pltpu.make_async_copy(sums.at[d, here], out_hbm.at[row_slice(1 - d, p)], y_out.at[p])

    def y_first(d, p):
        here = pl.ds(pl.multiple_of(p * rows, rows), rows)
        return line.copy(d, sums.at[1 - d, here], out_hbm.at[row_slice(d, p)], y_send.at[d, p], y_recv.at[d, p])

    def y_next(d, p):
        return line.copy(d, out_hbm.at[row_slice(d, p)], out_hbm.at[row_slice(d, p)], y_send.at[d, p], y_recv.at[d, p])

    def group_slices(g):
        return [pl.ds(pl.multiple_of(base + g * group_rows, group_rows), group_rows) for base in (0, half)]

    def product(g, unit):
        @pl.when(unit < up_tiles)
        def _():
            lanes = pl.ds(pl.multiple_of(unit * TILE, TILE), TILE)
            for k, group in enumerate(group_slices(g)):
                pre = jnp.dot(h[group, :], up[:, lanes], preferred_element_type=jnp.float32)
                act[k * group_rows:(k + 1) * group_rows, lanes] = jnp.square(jnp.maximum(pre, 0.0)).astype(jnp.bfloat16)

        @pl.when(unit == up_tiles)
        def _():
            for q in range(PER_GROUP):
                for d in range(2):

                    @pl.when(line.place[d] < line.last)
                    def _():
                        h_copy(d, g * PER_GROUP + q).wait_send()

        @pl.when((unit >= up_tiles) & (unit < up_tiles + down_tiles))
        def _():
            lanes = pl.ds(pl.multiple_of((unit - up_tiles) * TILE, TILE), TILE)
            for k, group in enumerate(group_slices(g)):
                part = jnp.dot(act[k * group_rows:(k + 1) * group_rows, :], down[:, lanes], preferred_element_type=jnp.float32)
                h[group, lanes] = part.astype(jnp.bfloat16)

    def step(t, _):
        for d in range(2):
            place = line.place[d]
            m = t - place

            @pl.when((m >= 0) & (m < PIECES))
            def _():
                @pl.when(place > 0)
                def _():
                    h_copy(d, m).wait_recv()

                @pl.when(place < line.last)
                def _():
                    h_copy(d, m).start()

            p = m - PIECES

            def finish(here, part_rows, rows_done, d=d, p=p):
                y_local(d, p, here).start()

            @pl.when((p >= 0) & (p < PIECES))
            def _():
                sum_step(line, d, p, rows, h, sums, send, recv, finish)

            q = m - 2 * PIECES

            @pl.when((q >= 0) & (q < PIECES))
            def _():
                @pl.when(place == 0)
                def _():
                    y_first(d, q).start()

                @pl.when(place > 0)
                def _():
                    y_next(d, q).wait_recv()

                    @pl.when(place < line.last)
                    def _():
                        y_next(d, q).start()

        @pl.when(t == first)
        def _():
            for load in loads:
                load.wait()

        k = t - first

        @pl.when((k >= 0) & (k < PIECES))
        def _():
            def units(u, _):
                product(k // PER_GROUP, (k % PER_GROUP) * per_step + u)
                return 0

            lax.fori_loop(0, per_step, units, 0)

        return 0

    lax.fori_loop(0, 3 * PIECES + line.last, step, 0)
    drain_sums(line, rows, h, sums, send, recv, lambda d, p, here: y_local(d, p, here).wait())

    def drain(p, _):
        for d in range(2):

            @pl.when(line.place[d] < line.last)
            def _():
                y_next(d, p).wait_send()

        return 0

    lax.fori_loop(0, PIECES, drain, 0)


def attend_reduce(n_tp, q_heads, seq_lens, qkv, k_rot, tables, gain, first_ctx, o_full, x_rows):
    seq_length, width = x_rows.shape
    half = seq_length // 2
    own = jax.ShapeDtypeStruct((half, width), jnp.bfloat16)
    any_spec = pl.BlockSpec(memory_space=pl.ANY)
    vmem_spec = pl.BlockSpec(memory_space=pltpu.VMEM)
    dma = pltpu.SemaphoreType.DMA
    return pl.pallas_call(
        functools.partial(attend_reduce_kernel, n_tp, q_heads),
        in_specs=[pl.BlockSpec(memory_space=pltpu.SMEM)] + [vmem_spec] * 6 + [any_spec] * 3,
        out_specs=[any_spec, any_spec],
        out_shape=[own, own],
        scratch_shapes=[
            pltpu.VMEM(o_full.shape, jnp.bfloat16),
            pltpu.VMEM((seq_length, width), jnp.bfloat16),
            pltpu.VMEM((2, half, width), jnp.bfloat16),
            pltpu.VMEM(first_ctx.shape, jnp.bfloat16),
            dma((2,)), dma, dma((2, PIECES)), dma((2, PIECES)), dma((PIECES,)), dma((PIECES,)),
        ],
        compiler_params=pltpu.CompilerParams(collective_id=0, has_side_effects=True, vmem_limit_bytes=60 << 20),
        cost_estimate=pl.CostEstimate(flops=150 * 10 ** 9, bytes_accessed=32 << 20, transcendentals=0),
        name="attend_reduce",
    )(seq_lens, qkv, k_rot, *tables, gain.reshape(1, width), first_ctx, o_full, x_rows)


def mlp_rows(n_tp, x_own, h_own, up_full, down_full):
    half, width = x_own.shape
    hidden = up_full.shape[1]
    any_spec = pl.BlockSpec(memory_space=pl.ANY)
    dma = pltpu.SemaphoreType.DMA
    return pl.pallas_call(
        functools.partial(mlp_kernel, n_tp),
        in_specs=[any_spec] * 4,
        out_specs=any_spec,
        out_shape=jax.ShapeDtypeStruct((2 * half, width), jnp.bfloat16),
        scratch_shapes=[
            pltpu.VMEM((width, hidden), jnp.bfloat16),
            pltpu.VMEM((hidden, width), jnp.bfloat16),
            pltpu.VMEM((2 * half, width), jnp.bfloat16),
            pltpu.VMEM((2, half, width), jnp.bfloat16),
            pltpu.VMEM((2 * half // PIECES * PER_GROUP, hidden), jnp.bfloat16),
            dma((2,)), dma((2,)),
        ] + [dma((2, PIECES))] * 6 + [dma((PIECES,))],
        compiler_params=pltpu.CompilerParams(collective_id=1, has_side_effects=True, vmem_limit_bytes=63 << 20),
        cost_estimate=pl.CostEstimate(flops=400 * 10 ** 9, bytes_accessed=64 << 20, transcendentals=0),
        name="mlp_rows",
    )(x_own, h_own, up_full, down_full)


def solution(mesh):
    batch_axes = ("dp", "fsdp")
    arg_specs = (P(batch_axes, None, None), P(batch_axes), P(None), P("fsdp", "tp", None), P("fsdp", "tp", None), P("fsdp", "tp", None), P("tp", None, "fsdp"), P(None), P("fsdp", "tp"), P("tp", "fsdp"))
    out_parts = (P(batch_axes, None, None), P(batch_axes, None, "tp", None), P(batch_axes, None, "tp", None))
    n_tp = mesh.shape["tp"]

    def layer_local(x_in, seq_lens, ln1_gain, w_q, w_k, w_v, w_o, ln2_gain, w_up, w_down):
        _, seq_length, width = x_in.shape
        q_heads, kv_heads, head_dim = w_q.shape[1], w_k.shape[1], w_k.shape[2]
        x_rows = x_in.reshape(seq_length, width)

        w_qkv = jnp.concatenate([w.reshape(w.shape[0], -1) for w in (w_q, w_k, w_v)], axis=1)
        qkv_full = lax.all_gather(w_qkv, "fsdp", axis=0, tiled=True)
        o_full = lax.all_gather(w_o.reshape(q_heads * head_dim, -1), "fsdp", axis=1, tiled=True)
        up_full = lax.all_gather(w_up, "fsdp", axis=0, tiled=True)
        down_full = lax.all_gather(w_down, "fsdp", axis=1, tiled=True)

        tables = rotary_tables(seq_length, head_dim)
        h_norm = layer_norm(x_rows, ln1_gain)
        qkv = jnp.dot(h_norm, qkv_full, preferred_element_type=jnp.float32).astype(jnp.bfloat16)
        first_ctx, k_rot = first_strips(qkv, seq_lens, tables, q_heads, kv_heads, head_dim)
        v_loc = qkv[:, (q_heads + kv_heads) * head_dim:]
        x_own, h_own = attend_reduce(n_tp, q_heads, seq_lens, qkv, k_rot, tables, ln2_gain, first_ctx, o_full, x_rows)
        out = mlp_rows(n_tp, x_own, h_own, up_full, down_full)

        y_out = out.reshape(1, seq_length, width)
        k_cache = k_rot.reshape(1, seq_length, kv_heads, head_dim)
        v_cache = v_loc.reshape(1, seq_length, kv_heads, head_dim)
        return y_out, k_cache, v_cache

    return jax.shard_map(layer_local, mesh=mesh, in_specs=arg_specs, out_specs=out_parts, check_vma=False)
```

profile of v0, /device:TPU:0, one launch (start us, length us, event | category | flops | bytes accessed | tf_op | source)
XLA Modules:
  0.0 790.5 jit_solution(17736212347190837931)
XLA Ops:
  7.2 1.9 copy.21
  9.1 1.2 copy_bitcast_fusion.1
  10.3 1.6 pad_maximum_fusion
  11.9 0.7 all-gather.7.cloned.1.call-update
  12.7 0.7 all-gather.9.cloned.1.call-update
  13.4 0.5 all-gather.11.cloned.1.call-update
  14.6 0.1 pad.5.clone
  14.7 0.1 pad.8.clone
  14.8 6.3 convert_reduce_fusion
  21.1 8.0 %fusion.2 = f32[2048]{0:T(1024)S(1)} fusion(f32[2048]{0:T(1024)S(1)} %broadcast_multiply_fusion, bf16[1,2048,3072]{2,1,0:T(8,128)(2,1)} %param.10), kind=kLoop, calls=%fused_computation.4 | loop fusion | flops 25163776 | bytes 12599296 | tf_op jit(solution)/shard_map/reduce_sum | solution.py:22
  29.1 0.6 reshape.55.gain_ref
  29.7 3.9 fusion.15
  33.7 1.9 maximum_maximum_fusion.2
  35.5 43.8 %all-gather.5.cloned.1.call-done = bf16[3072,1536]{1,0:T(8,128)(2,1)} async-done(((bf16[768,1536]{1,0:T(8,128)(2,1)}), bf16[3072,1536]{1,0:T(8,128)(2,1)}) %all-gather.5.cloned.1.call-update) | async-done | bytes 9437200 | tf_op jit(solution)/shard_map/all_gather | solution.py:514
  79.4 25.4 %fusion.10.q_ref.k_ref.v_ref.qkv = bf16[2048,1536]{1,0:T(8,128)(2,1)S(1)} fusion(bf16[3072,1536]{1,0:T(8,128)(2,1)} %all-gather.5.cloned.1.call-done, f32[3072]{0:T(1024)S(1)} %convert_add_fusion, f32[2048]{0:T(1024)S(1)} %add_rsqrt_fusion, f32[2048]{0:T(1024)S(1)} %broadcast_multiply_fusion, bf16[1,2048,3072]{2,1,0:T(8,128)(2,1)} %param.10), kind=kOutput, calls=%fused_computation.11 | convolution fusion | flops 19361955840 | bytes 28340224 | tf_op jit(solution)/shard_map/dot_general | solution.py:521
  104.8 2.7 copy-done.5
  107.6 1.1 reshape.59
  108.7 1.2 copy-done.3
  109.9 18.7 %first_strips.1 = (bf16[512,1024]{1,0:T(8,128)(2,1)S(1)}, bf16[2048,256]{1,0:T(8,128)(2,1)S(1)}) custom-call(s32[1]{0:T(128)S(6)} %copy.23.len_ref, bf16[2048,1536]{1,0:T(8,128)(2,1)} %copy-done.5, bf16[2048,1536]{1,0:T(8,128)(2,1)} %copy-done.5, bf16[2048,1536]{1,0:T(8,128)(2,1)} %copy-done.5, f32[2048,128]{1,0:T(8,128)S(1)} %copy-done.3, ...), custom_call_target="tpu_custom_call" | custom-call | flops 15000000512 | bytes 12582912 | tf_op jit(solution)/shard_map/first_strips/pallas_call | solution.py:110
  128.6 1.0 copy-done.4
  129.6 1.3 reshape.58
  130.9 195.8 %attend_reduce.1 = (bf16[1024,3072]{1,0:T(8,128)(2,1)}, bf16[1024,3072]{1,0:T(8,128)(2,1)}) custom-call(s32[1]{0:T(128)S(6)} %copy.23.len_ref, bf16[2048,1536]{1,0:T(8,128)(2,1)} %copy-done.5, bf16[2048,256]{1,0:T(8,128)(2,1)} %copy-done, f32[2048,128]{1,0:T(8,128)} %get-tuple-element.18.qc_ref.kc_ref.keep, f32[2048,128]{1,0:T(8,128)} %copy-done.2, ...), custom_call_target="tpu_custom_call" | custom-call | flops 149999992832 | bytes 33554432 | tf_op jit(solution)/shard_map/attend_reduce/pallas_call | solution.py:460
  326.8 446.6 %mlp_rows.1 = bf16[2048,3072]{1,0:T(8,128)(2,1)} custom-call(bf16[1024,3072]{1,0:T(8,128)(2,1)} %get-tuple-element.9.x_own_hbm, bf16[1024,3072]{1,0:T(8,128)(2,1)} %get-tuple-element.10.h_own_hbm, bf16[3072,2304]{1,0:T(8,128)(2,1)} %all-gather.9.cloned.1.call-done.up_hbm, bf16[2304,3072]{1,0:T(8,128)(2,1)} %all-gather.11.cloned.1.call-done.down_hbm), custom_call_target="tpu_custom_call" | custom-call | flops 399999991808 | bytes 67108864 | tf_op jit(solution)/shard_map/mlp_rows/pallas_call | solution.py:483
  773.4 10.5 %copy.24 = bf16[1,2048,3072]{2,1,0:T(8,128)(2,1)} copy(bf16[1,2048,3072]{2,1,0:T(8,128)(2,1)} %bitcast.21) | data formatting | bytes 25165824
  (29 shorter events, 0.5 us)
Async XLA Ops:
  7.2 72.2 %all-gather.5.cloned.1.call-start = ((), (), s32[]{:S(2)}) async-start(), calls=%async_computation | async-start | bytes 11796480 | tf_op jit(solution)/shard_map/all_gather | solution.py:514
  11.9 119.0 %all-gather.7.cloned.1.call-start = ((), (), s32[]{:S(2)}) async-start(), calls=%async_computation.1 | async-start | bytes 7864320 | tf_op jit(solution)/shard_map/all_gather | solution.py:515
  12.7 314.1 %all-gather.9.cloned.1.call-start = ((), (), s32[]{:S(2)}) async-start(), calls=%async_computation.2 | async-start | bytes 17694720 | tf_op jit(solution)/shard_map/all_gather | solution.py:516
  13.4 313.4 %all-gather.11.cloned.1.call-start = ((), (), s32[]{:S(2)}) async-start(), calls=%async_computation.3 | async-start | bytes 17694720 | tf_op jit(solution)/shard_map/all_gather | solution.py:517
  21.1 8.0 %copy-start.6 = (bf16[3072]{0:T(1024)(128)(2,1)S(1)}, bf16[3072]{0:T(1024)(128)(2,1)}, u32[]{:S(2)}) copy-start(bf16[3072]{0:T(1024)(128)(2,1)} %param.17) | copy-start | bytes 18436
  21.1 8.6 %copy-start.7 = (bf16[3072]{0:T(1024)(128)(2,1)S(1)}, bf16[3072]{0:T(1024)(128)(2,1)}, u32[]{:S(2)}) copy-start(bf16[3072]{0:T(1024)(128)(2,1)} %param.12) | copy-start | bytes 18436
  35.5 73.2 %copy-start.1 = (f32[2048,128]{1,0:T(8,128)}, f32[2048,128]{1,0:T(8,128)S(1)}, u32[]{:S(2)}) copy-start(f32[2048,128]{1,0:T(8,128)S(1)} %get-tuple-element.11.qh_ref.kh_ref.from_high) | copy-start | bytes 3145732
  35.5 73.2 %copy-start.2 = (f32[2048,128]{1,0:T(8,128)}, f32[2048,128]{1,0:T(8,128)S(1)}, u32[]{:S(2)}) copy-start(f32[2048,128]{1,0:T(8,128)S(1)} %get-tuple-element.12.ql_ref.kl_ref.from_low) | copy-start | bytes 3145732
  104.8 2.7 copy-start.5
  108.7 1.2 copy-start.3
  128.6 1.0 copy-start.4
  129.6 1.4 copy-start
Sparse Core Ops, SparseCore 0:
  12.0 67.3 all-gather.4
  80.9 46.3 all-gather.6
  128.9 91.8 all-gather.8
  222.2 91.8 all-gather.10
where the time goes:
time: 793 us; the launch traced here: 790 us
  Pallas kernels  661 us (83%)
  waiting for transfers between devices  45.8 us (6%)
  matrix products  25.4 us (3%)
  local copies, waits for them, and re-layouts  21.9 us (3%)
  other arithmetic  21.6 us (3%)
  between operations  14.6 us (2%)
    pallas_call x1, Pallas kernels, mlp_rows(): pl.pallas_call(functools.partial(mlp_kernel, n_tp), in_specs=[any_spec] *...  447 us
    pallas_call x1, Pallas kernels, attend_reduce(): pl.pallas_call(functools.partial(attend_reduce_kernel, n_tp, q_heads), in...  196 us
    all_gather x1, waiting for transfers between devices, layer_local(): qkv_full = lax.all_gather(w_qkv, 'fsdp', axis=0, tiled=True)  43.8 us
    dot_general x1, matrix products, layer_local(): jnp.dot(h_norm, qkv_full, preferred_element_type=jnp.float32)  25.4 us
    pallas_call x1, Pallas kernels, first_strips(): pl.pallas_call(first_strips_kernel, grid_spec=pltpu.PrefetchScalarGridSpe...  18.7 us
    unnamed x18, local copies, waits for them, and re-layouts  17.4 us
  transfers between devices with their start and end apart: 4, of which 1 were waited for; matrix products, arithmetic and copies ran while one was open for 6% of the time, Pallas kernels for 27%

commit v1 on v0

--- a/solution.py
+++ b/solution.py
@@ -9,6 +9,7 @@
 
 EPS = 1e-5
 ROPE_BASE = 10000.0
+LOG2_E = 1.4426950408889634
 PIECES = 16
 PER_GROUP = 4
 TILE = 256
@@ -48,7 +49,7 @@
 
 def strip_attention(q_rot, k_blocks, v_blocks, row0, seq_len):
     head_dim = q_rot[0].shape[1]
-    scale = head_dim ** -0.5
+    scale = head_dim ** -0.5 * LOG2_E
 
     def step(diagonal, kb, carry):
         start = pl.multiple_of(kb * KBLK, KBLK)
@@ -65,8 +66,8 @@
             if diagonal:
                 s = jnp.where(causal, s, -1e30)
             m_new = jnp.maximum(m_old, jnp.max(s, axis=1, keepdims=True))
-            corr = jnp.exp(m_old - m_new)
-            p = jnp.exp(s - m_new)
+            corr = jnp.exp2(m_old - m_new)
+            p = jnp.exp2(s - m_new)
             l_new = l_old * corr + jnp.sum(p, axis=1, keepdims=True)
             acc = acc * corr + jnp.dot(p.astype(jnp.bfloat16), v_blk, preferred_element_type=jnp.float32)
             out.append((m_new, l_new, acc))
@@ -250,19 +251,19 @@
 
         lax.fori_loop(0, part.shape[1] // TILE, tile, 0)
 
-    def attend(strip, k, kv):
+    def attend(strip, k, kv, heads):
         row0 = pl.multiple_of(k * half + strip * QBLK, QBLK)
         q_rows = pl.ds(row0, QBLK)
         tables = (keep[q_rows, :], from_low[q_rows, :], from_high[q_rows, :])
         context = strip_attention(
-            [rotate(qkv[q_rows, lanes_of(kv * group + h, head_dim)], *tables) for h in range(group)],
+            [rotate(qkv[q_rows, lanes_of(kv * group + h, head_dim)], *tables) for h in heads],
             lambda start: k_rot[pl.ds(start, KBLK), lanes_of(kv, head_dim)],
             lambda start: qkv[pl.ds(start, KBLK), lanes_of(q_heads + kv_heads + kv, head_dim)],
             row0,
             seq_len,
         )
-        for h in range(group):
-            ctx[pl.ds(pl.multiple_of(k * QBLK, QBLK), QBLK), lanes_of(kv * group + h, head_dim)] = context[h]
+        for h, context_rows in zip(heads, context):
+            ctx[pl.ds(pl.multiple_of(k * QBLK, QBLK), QBLK), lanes_of(kv * group + h, head_dim)] = context_rows
 
     output_product(0)
     own_copies(line, half, lambda d, row: own(d, row).wait())
@@ -287,18 +288,17 @@
             def _():
                 sum_step(line, d, p, rows, part, sums, send, recv, finish)
 
-        strip = t // per_strip + 1
-        unit = t % per_strip
-
-        @pl.when(strip < strips)
-        def _():
-            @pl.when(unit < 2 * kv_heads)
-            def _():
-                attend(strip, unit // kv_heads, unit % kv_heads)
-
-            @pl.when(unit == per_strip - 1)
-            def _():
-                output_product(strip)
+            strip = t // per_strip + 1
+            unit = t % per_strip
+
+            @pl.when((strip < strips) & (unit < 2 * kv_heads))
+            def _():
+                heads = range(group // 2 * d, group // 2 + (group - group // 2) * d)
+                attend(strip, unit // kv_heads, unit % kv_heads, heads)
+
+        @pl.when((strip < strips) & (unit == per_strip - 1))
+        def _():
+            output_product(strip)
 
         return 0
 
@@ -329,11 +329,11 @@
             pltpu.make_async_copy(h_own_hbm, h.at[pl.ds(row, half)], own_sem.at[1]),
         )
 
-    own_copies(line, half, lambda d, row: [c.start() for c in own(d, row)])
+    own_copies(line, half, lambda d, row: [c.start() for c in reversed(own(d, row))])
     for load in loads:
         load.start()
     line.meet()
-    own_copies(line, half, lambda d, row: [c.wait() for c in own(d, row)])
+    own_copies(line, half, lambda d, row: own(d, row)[1].wait())
 
     def row_slice(d, p):
         return pl.ds(pl.multiple_of(line.row_base[d] + p * rows, rows), rows)
@@ -420,6 +420,7 @@
 
         @pl.when(t == first)
         def _():
+            own_copies(line, half, lambda d, row: own(d, row)[0].wait())
             for load in loads:
                 load.wait()
 

time: 793 us -> 788 us (level)
  no operation moved by 1% of the time
where the time goes in v1:
time: 788 us
  Pallas kernels  658 us (84%)
  waiting for transfers between devices  45.8 us (6%)
  matrix products  25.4 us (3%)
  local copies, waits for them, and re-layouts  21.9 us (3%)
  other arithmetic  21.6 us (3%)
  between operations  14.6 us (2%)
    pallas_call x1, Pallas kernels, mlp_rows(): pl.pallas_call(functools.partial(mlp_kernel, n_tp), in_specs=[any_spec] *...  443 us
    pallas_call x1, Pallas kernels, attend_reduce(): pl.pallas_call(functools.partial(attend_reduce_kernel, n_tp, q_heads), in...  196 us
    all_gather x1, waiting for transfers between devices, layer_local(): qkv_full = lax.all_gather(w_qkv, 'fsdp', axis=0, tiled=True)  43.8 us
    dot_general x1, matrix products, layer_local(): jnp.dot(h_norm, qkv_full, preferred_element_type=jnp.float32)  25.4 us
    pallas_call x1, Pallas kernels, first_strips(): pl.pallas_call(first_strips_kernel, grid_spec=pltpu.PrefetchScalarGridSpe...  18.6 us
    unnamed x18, local copies, waits for them, and re-layouts  17.4 us
  transfers between devices with their start and end apart: 4, of which 1 were waited for; matrix products, arithmetic and copies ran while one was open for 6% of the time, Pallas kernels for 27%

profile of v1, /device:TPU:0, one launch (start us, length us, event | category | flops | bytes accessed | tf_op | source)
XLA Modules:
  0.0 787.6 jit_solution(13748784013821890650)
XLA Ops:
  7.2 1.9 copy.21
  9.1 1.2 copy_bitcast_fusion.1
  10.3 1.6 pad_maximum_fusion
  11.9 0.7 all-gather.7.cloned.1.call-update
  12.7 0.7 all-gather.9.cloned.1.call-update
  13.4 0.5 all-gather.11.cloned.1.call-update
  14.6 0.1 pad.5.clone
  14.7 0.1 pad.8.clone
  14.8 6.3 convert_reduce_fusion
  21.1 8.0 %fusion.2 = f32[2048]{0:T(1024)S(1)} fusion(f32[2048]{0:T(1024)S(1)} %broadcast_multiply_fusion, bf16[1,2048,3072]{2,1,0:T(8,128)(2,1)} %param.10), kind=kLoop, calls=%fused_computation.4 | loop fusion | flops 25163776 | bytes 12599296 | tf_op jit(solution)/shard_map/reduce_sum | solution.py:23
  29.1 0.6 reshape.55.gain_ref
  29.7 3.9 fusion.15
  33.7 1.9 maximum_maximum_fusion.2
  35.5 43.8 %all-gather.5.cloned.1.call-done = bf16[3072,1536]{1,0:T(8,128)(2,1)} async-done(((bf16[768,1536]{1,0:T(8,128)(2,1)}), bf16[3072,1536]{1,0:T(8,128)(2,1)}) %all-gather.5.cloned.1.call-update) | async-done | bytes 9437200 | tf_op jit(solution)/shard_map/all_gather | solution.py:515
  79.4 25.4 %fusion.10.q_ref.k_ref.v_ref.qkv = bf16[2048,1536]{1,0:T(8,128)(2,1)S(1)} fusion(bf16[3072,1536]{1,0:T(8,128)(2,1)} %all-gather.5.cloned.1.call-done, f32[3072]{0:T(1024)S(1)} %convert_add_fusion, f32[2048]{0:T(1024)S(1)} %add_rsqrt_fusion, f32[2048]{0:T(1024)S(1)} %broadcast_multiply_fusion, bf16[1,2048,3072]{2,1,0:T(8,128)(2,1)} %param.10), kind=kOutput, calls=%fused_computation.11 | convolution fusion | flops 19361955840 | bytes 28340224 | tf_op jit(solution)/shard_map/dot_general | solution.py:522
  104.8 2.7 copy-done.5
  107.6 1.1 reshape.59
  108.7 1.2 copy-done.3
  109.9 18.6 %first_strips.1 = (bf16[512,1024]{1,0:T(8,128)(2,1)S(1)}, bf16[2048,256]{1,0:T(8,128)(2,1)S(1)}) custom-call(s32[1]{0:T(128)S(6)} %copy.23.len_ref, bf16[2048,1536]{1,0:T(8,128)(2,1)} %copy-done.5, bf16[2048,1536]{1,0:T(8,128)(2,1)} %copy-done.5, bf16[2048,1536]{1,0:T(8,128)(2,1)} %copy-done.5, f32[2048,128]{1,0:T(8,128)S(1)} %copy-done.3, ...), custom_call_target="tpu_custom_call" | custom-call | flops 15000000512 | bytes 12582912 | tf_op jit(solution)/shard_map/first_strips/pallas_call | solution.py:111
  128.6 1.0 copy-done.4
  129.6 1.3 reshape.58
  130.9 196.2 %attend_reduce.1 = (bf16[1024,3072]{1,0:T(8,128)(2,1)}, bf16[1024,3072]{1,0:T(8,128)(2,1)}) custom-call(s32[1]{0:T(128)S(6)} %copy.23.len_ref, bf16[2048,1536]{1,0:T(8,128)(2,1)} %copy-done.5, bf16[2048,256]{1,0:T(8,128)(2,1)} %copy-done, f32[2048,128]{1,0:T(8,128)} %get-tuple-element.18.qc_ref.kc_ref.keep, f32[2048,128]{1,0:T(8,128)} %copy-done.2, ...), custom_call_target="tpu_custom_call" | custom-call | flops 149999992832 | bytes 33554432 | tf_op jit(solution)/shard_map/attend_reduce/pallas_call | solution.py:461
  327.1 443.3 %mlp_rows.1 = bf16[2048,3072]{1,0:T(8,128)(2,1)} custom-call(bf16[1024,3072]{1,0:T(8,128)(2,1)} %get-tuple-element.9.x_own_hbm, bf16[1024,3072]{1,0:T(8,128)(2,1)} %get-tuple-element.10.h_own_hbm, bf16[3072,2304]{1,0:T(8,128)(2,1)} %all-gather.9.cloned.1.call-done.up_hbm, bf16[2304,3072]{1,0:T(8,128)(2,1)} %all-gather.11.cloned.1.call-done.down_hbm), custom_call_target="tpu_custom_call" | custom-call | flops 399999991808 | bytes 67108864 | tf_op jit(solution)/shard_map/mlp_rows/pallas_call | solution.py:484
  770.5 10.5 %copy.24 = bf16[1,2048,3072]{2,1,0:T(8,128)(2,1)} copy(bf16[1,2048,3072]{2,1,0:T(8,128)(2,1)} %bitcast.21) | data formatting | bytes 25165824
  (29 shorter events, 0.5 us)
Async XLA Ops:
  7.2 72.2 %all-gather.5.cloned.1.call-start = ((), (), s32[]{:S(2)}) async-start(), calls=%async_computation | async-start | bytes 11796480 | tf_op jit(solution)/shard_map/all_gather | solution.py:515
  11.9 119.0 %all-gather.7.cloned.1.call-start = ((), (), s32[]{:S(2)}) async-start(), calls=%async_computation.1 | async-start | bytes 7864320 | tf_op jit(solution)/shard_map/all_gather | solution.py:516
  12.7 314.5 %all-gather.9.cloned.1.call-start = ((), (), s32[]{:S(2)}) async-start(), calls=%async_computation.2 | async-start | bytes 17694720 | tf_op jit(solution)/shard_map/all_gather | solution.py:517
  13.4 313.8 %all-gather.11.cloned.1.call-start = ((), (), s32[]{:S(2)}) async-start(), calls=%async_computation.3 | async-start | bytes 17694720 | tf_op jit(solution)/shard_map/all_gather | solution.py:518
  21.1 8.0 %copy-start.6 = (bf16[3072]{0:T(1024)(128)(2,1)S(1)}, bf16[3072]{0:T(1024)(128)(2,1)}, u32[]{:S(2)}) copy-start(bf16[3072]{0:T(1024)(128)(2,1)} %param.17) | copy-start | bytes 18436
  21.1 8.6 %copy-start.7 = (bf16[3072]{0:T(1024)(128)(2,1)S(1)}, bf16[3072]{0:T(1024)(128)(2,1)}, u32[]{:S(2)}) copy-start(bf16[3072]{0:T(1024)(128)(2,1)} %param.12) | copy-start | bytes 18436
  35.5 73.2 %copy-start.1 = (f32[2048,128]{1,0:T(8,128)}, f32[2048,128]{1,0:T(8,128)S(1)}, u32[]{:S(2)}) copy-start(f32[2048,128]{1,0:T(8,128)S(1)} %get-tuple-element.11.qh_ref.kh_ref.from_high) | copy-start | bytes 3145732
  35.5 73.2 %copy-start.2 = (f32[2048,128]{1,0:T(8,128)}, f32[2048,128]{1,0:T(8,128)S(1)}, u32[]{:S(2)}) copy-start(f32[2048,128]{1,0:T(8,128)S(1)} %get-tuple-element.12.ql_ref.kl_ref.from_low) | copy-start | bytes 3145732
  104.8 2.7 copy-start.5
  108.7 1.2 copy-start.3
  128.6 1.0 copy-start.4
  129.6 1.4 copy-start
Sparse Core Ops, SparseCore 0:
  12.0 67.3 all-gather.4
  80.9 46.3 all-gather.6
  128.9 91.8 all-gather.8
  222.2 91.8 all-gather.10
